TPU v7x, 32 devices: a whole 2x2x4 slice. The times are simulated.
32 devices in a mesh: row: 4 (over y, x), col: 8 (over z, core).
Axes of the slice: x: 2, y: 2, z: 4, core: 2. Of those that a mesh axis runs over, the one named last changes fastest.
Arguments:
- dense_in: bfloat16 [512, 28672], P('col', 'row'), may hold values from -6 to 6
- pruned_in: bfloat16 [512, 28672], P('col', 'row'), may hold values from -6 to 6
- weight: bfloat16 [28672, 8192], P('row', 'col'), may hold values from -0.03125 to 0.03125
- keep_bits: int32 [512, 28672], P('col', 'row'), may hold values from 0 to 65535
Outputs:
- gram_tile: float32 [8192, 8192], P('row', 'col')
- cross_tile: float32 [8192, 8192], P('row', 'col')
Inputs may be any that keep to these rules, and one draw needn't show every extreme that they name: `keep_bits`: each word holds 16 independent flags, each 1 with probability one half.
All inputs are finite; a program needn't handle non-finite values.
Results may differ from a plain program's by a relative error of at most 0.0039.
Values may be sent and summed in bfloat16 or wider, within the bound.
A program may use at most 128 MiB of HBM per device.

v0:
```python
import functools

import jax
import jax.numpy as jnp
from jax import lax
from jax.experimental import pallas as pl
from jax.experimental.pallas import tpu as pltpu
from jax.sharding import PartitionSpec as P

MESH = pl.DeviceIdType.MESH
CORES = 2
FLAG_BITS = 16
HALF_BITS = 8


def block_of(size, choices):
    for choice in choices:
        if size % choice == 0:
            return choice
    return size


def gather_kernel(
    n_row, n_col,
    pruned_in, dense_in, weight, keep,
    cols, panels,
    xs, ws, flags, pick, part, heard, piece,
    weight_sem, keep_sem, own_sem, x_recv, left_send, right_send, mate_send,
    sum_send, sum_recv, col_send, col_recv, col_own,
    panel_send, panel_recv, panel_own, pair_send, pair_recv,
):
    rows, depth = pruned_in.shape
    features = weight.shape[1]
    words = keep.shape[0]
    line = n_col // CORES
    per_row = n_col // n_row
    together = CORES * rows
    share = together // n_row
    row, col = lax.axis_index("row"), lax.axis_index("col")
    z, core = col // CORES, lax.rem(col, CORES)
    other = 1 - core
    mate = (row, z * CORES + other)
    home = col // per_row
    slot = lax.rem(col, per_row)

    barrier = pltpu.get_barrier_semaphore()
    for d in range(n_row):
        for e in range(n_col):
            if d or e:
                peer = (lax.rem(row + d, n_row), lax.rem(col + e, n_col))
                pl.semaphore_signal(barrier, inc=1, device_id=peer, device_id_type=MESH)

    chunk = block_of(depth, (512, 256, 128))
    chunks = depth // chunk

    def load_chunk(i):
        at = pl.ds(pl.multiple_of(i * chunk, chunk), chunk)
        return pltpu.make_async_copy(weight.at[at], ws.at[1, at], weight_sem.at[i])

    load_keep = pltpu.make_async_copy(keep, flags, keep_sem)
    load_keep.start()

    @pl.loop(0, chunks)
    def _(i):
        load_chunk(i).start()

    sources = (pruned_in, dense_in)

    def half(q, which):
        return pl.ds(pl.multiple_of(which * rows, rows), rows)

    def own_copy(m):
        return pltpu.make_async_copy(sources[m], xs.at[m, z, half(z, core)], own_sem.at[m])

    for m in range(2):
        own_copy(m).start()

    def x_copy(m, q, which, source, target, send):
        return pltpu.make_async_remote_copy(
            src_ref=source,
            dst_ref=xs.at[m, q, half(q, which)],
            send_sem=send,
            recv_sem=x_recv.at[m, q, which],
            device_id=target,
            device_id_type=MESH,
        )

    def block(m, q):
        return xs.at[m, q, half(q, core)]

    def to_left(m, q, source):
        return x_copy(m, q, core, source, (row, col - CORES), left_send.at[m, q])

    def to_right(m, q, source):
        return x_copy(m, q, core, source, (row, col + CORES), right_send.at[m, q])

    def to_mate(m, q, source):
        return x_copy(m, q, core, source, mate, mate_send.at[m, q])

    pl.semaphore_wait(barrier, n_row * n_col - 1)
    for m in range(2):
        @pl.when(z > 0)
        def _():
            to_left(m, z, sources[m]).start()

        @pl.when(z < line - 1)
        def _():
            to_right(m, z, sources[m]).start()

    for m in range(2):
        to_mate(m, z, sources[m]).start()

    w_at = lax.broadcasted_iota(jnp.int32, (2 * words, features), 0)
    f_at = lax.broadcasted_iota(jnp.int32, (2 * words, features), 1)
    high = jnp.where(w_at >= words, 1, 0)
    match = (w_at - high * words == f_at // FLAG_BITS) & (high == lax.rem(f_at, FLAG_BITS) // HALF_BITS)
    pick[...] = jnp.where(match, 1.0, 0.0).astype(jnp.bfloat16)
    lane = lax.broadcasted_iota(jnp.int32, (1, features), 1)
    bit = jnp.left_shift(jnp.ones_like(lane), lax.rem(lane, HALF_BITS))
    tile = block_of(chunk, (256, 128))
    load_keep.wait()

    @pl.loop(0, chunks)
    def _(i):
        load_chunk(i).wait()

        @pl.loop(0, chunk // tile)
        def _(j):
            start = pl.multiple_of(i * chunk + j * tile, tile)
            word = flags[:, pl.ds(start, tile)]
            low = (word & 255).astype(jnp.float32)
            top = (jnp.right_shift(word, HALF_BITS) & 255).astype(jnp.float32)
            halves = jnp.concatenate([low, top], 0).T.astype(jnp.bfloat16)
            spread = jnp.dot(halves, pick[...], preferred_element_type=jnp.float32)
            kept = jnp.where((spread.astype(jnp.int32) & bit) != 0, 1.0, 0.0)
            ws[0, pl.ds(start, tile), :] = ws[1, pl.ds(start, tile), :] * kept.astype(jnp.bfloat16)

    def position(s, side):
        return z + s * (1 - 2 * side)

    def present(s, side, q):
        return (q >= 0) & (q < line) & ((s > 0) | (side == 0))

    def arrive(m, s):
        @pl.loop(0, 2)
        def _(side):
            q = position(s, side)

            @pl.when(present(s, side, q) & (s > 0))
            def _():
                to_mate(m, q, block(m, q)).wait_recv()

                @pl.when((side == 0) & (z > 0))
                def _():
                    to_left(m, q, block(m, q)).start()

                @pl.when((side == 1) & (z < line - 1))
                def _():
                    to_right(m, q, block(m, q)).start()

                to_mate(m, q, block(m, q)).start()

    def sum_copy(m, q, d):
        target = lax.rem(row + d, n_row)
        at = pl.ds(pl.multiple_of(target * share, share), share)
        return pltpu.make_async_remote_copy(
            src_ref=part.at[m, q, at],
            dst_ref=heard.at[m, q, d - 1],
            send_sem=sum_send.at[m, q, d - 1],
            recv_sem=sum_recv.at[m, q, d - 1],
            device_id=(target, col),
            device_id_type=MESH,
        )

    wide = block_of(features, (512, 256, 128))

    def multiply(m, s):
        @pl.loop(0, 2)
        def _(side):
            q = position(s, side)

            @pl.when(present(s, side, q))
            def _():
                x_copy(m, q, other, block(m, q), mate, mate_send.at[m, q]).wait_recv()

                @pl.loop(0, features // wide)
                def _(n):
                    at = pl.ds(pl.multiple_of(n * wide, wide), wide)
                    part[m, q, :, at] = jnp.dot(xs[m, q], ws[m, :, at], preferred_element_type=jnp.float32)

                @pl.when(m == 1)
                def _():
                    part[1, q] = part[1, q] - part[0, q]

                for d in range(1, n_row):
                    sum_copy(m, q, d).start()

    def token_rows(q, which):
        return pl.ds(pl.multiple_of(q * together + which * share, share), share)

    def slot_columns(j):
        return pl.ds(pl.multiple_of(j * features, features), features)

    def col_copy(q, d):
        return pltpu.make_async_remote_copy(
            src_ref=piece.at[0, q],
            dst_ref=cols.at[token_rows(q, row)],
            send_sem=col_send.at[q, d - 1],
            recv_sem=col_recv.at[q, d - 1],
            device_id=(lax.rem(row + d, n_row), col),
            device_id_type=MESH,
        )

    def col_local(q):
        return pltpu.make_async_copy(piece.at[0, q], cols.at[token_rows(q, row)], col_own.at[q])

    def panel_copy(m, q, j, source_row, at):
        return pltpu.make_async_remote_copy(
            src_ref=piece.at[m, q],
            dst_ref=panels.at[m, token_rows(q, source_row), slot_columns(j)],
            send_sem=panel_send.at[m, q, at],
            recv_sem=panel_recv.at[m, q, j, source_row],
            device_id=(home, at * CORES + core),
            device_id_type=MESH,
        )

    def panel_local(m, q):
        return pltpu.make_async_copy(
            piece.at[m, q], panels.at[m, token_rows(q, row), slot_columns(slot)], panel_own.at[m, q]
        )

    def is_self(at):
        return (at == z) & (row == home)

    def settle(m, s):
        @pl.loop(0, 2)
        def _(side):
            q = position(s, side)

            @pl.when(present(s, side, q))
            def _():
                total = part[m, q, pl.ds(pl.multiple_of(row * share, share), share), :]
                for d in range(1, n_row):
                    sum_copy(m, q, d).wait_recv()
                    total = total + heard[m, q, d - 1]
                piece[m, q] = total.astype(jnp.bfloat16)

                @pl.loop(0, line)
                def _(at):
                    @pl.when(is_self(at))
                    def _():
                        panel_local(m, q).start()

                    @pl.when(jnp.logical_not(is_self(at)))
                    def _():
                        panel_copy(m, q, slot, row, at).start()

                @pl.when(m == 0)
                def _():
                    col_local(q).start()
                    for d in range(1, n_row):
                        col_copy(q, d).start()

    for m in range(2):
        own_copy(m).wait()

    @pl.loop(0, 2 * line)
    def _(t):
        s, m = t // 2, lax.rem(t, 2)
        arrive(m, s)
        multiply(m, s)

        @pl.when(t > 0)
        def _():
            settle(1 - m, (t - 1) // 2)

    settle(1, line - 1)

    def comes_here(j):
        return lax.rem(row * per_row + j, CORES) == core

    def panel_rows(q):
        return pl.ds(pl.multiple_of(q * together, together), together)

    def pair_copy(m, q, j):
        part_of = panels.at[m, panel_rows(q), slot_columns(j)]
        return pltpu.make_async_remote_copy(
            src_ref=part_of,
            dst_ref=part_of,
            send_sem=pair_send.at[m, q, j],
            recv_sem=pair_recv.at[m, q, j],
            device_id=mate,
            device_id_type=MESH,
        )

    @pl.loop(0, 2 * line)
    def _(t):
        s, m = t // 2, lax.rem(t, 2)

        @pl.loop(0, 2)
        def _(side):
            for j in range(per_row):
                origin = (row * per_row + j) // CORES
                q = origin + s * (1 - 2 * side)

                @pl.when(present(s, side, q) & comes_here(j))
                def _():
                    for source_row in range(n_row):
                        here = (origin == z) & (row == source_row)

                        @pl.when(here)
                        def _():
                            panel_local(m, q).wait()

                        @pl.when(jnp.logical_not(here))
                        def _():
                            panel_copy(m, q, j, source_row, z).wait_recv()

                    pair_copy(m, q, j).start()

    @pl.loop(0, line)
    def _(q):
        col_local(q).wait()
        for d in range(1, n_row):
            col_copy(q, d).wait_recv()
            col_copy(q, d).wait_send()
        for m in range(2):
            for j in range(per_row):
                @pl.when(comes_here(j))
                def _():
                    pair_copy(m, q, j).wait_send()

                @pl.when(jnp.logical_not(comes_here(j)))
                def _():
                    pair_copy(m, q, j).wait_recv()

            @pl.loop(0, line)
            def _(at):
                @pl.when(jnp.logical_not(is_self(at)))
                def _():
                    panel_copy(m, q, slot, row, at).wait_send()

            for d in range(1, n_row):
                sum_copy(m, q, d).wait_send()
            to_mate(m, q, block(m, q)).wait_send()

            @pl.when((z > 0) & (q >= z))
            def _():
                to_left(m, q, block(m, q)).wait_send()

            @pl.when((z < line - 1) & (q <= z))
            def _():
                to_right(m, q, block(m, q)).wait_send()


def gather(pruned_in, dense_in, weight, keep_bits):
    n_row, n_col = lax.axis_size("row"), lax.axis_size("col")
    rows, depth = pruned_in.shape
    features = weight.shape[1]
    words = keep_bits.shape[0]
    line, per_row = n_col // CORES, n_col // n_row
    together, tokens = CORES * rows, n_col * rows
    share = together // n_row
    dma = pltpu.SemaphoreType.DMA
    chunks = depth // block_of(depth, (512, 256, 128))
    anywhere = pl.BlockSpec(memory_space=pl.ANY)
    return pl.pallas_call(
        functools.partial(gather_kernel, n_row, n_col),
        out_shape=(
            jax.ShapeDtypeStruct((tokens, features), jnp.bfloat16),
            jax.ShapeDtypeStruct((2, tokens, per_row * features), jnp.bfloat16),
        ),
        in_specs=[anywhere] * 4,
        out_specs=(anywhere, anywhere),
        scratch_shapes=[
            pltpu.VMEM((2, line, together, depth), jnp.bfloat16),
            pltpu.VMEM((2, depth, features), jnp.bfloat16),
            pltpu.VMEM((words, depth), jnp.int32),
            pltpu.VMEM((2 * words, features), jnp.bfloat16),
            pltpu.VMEM((2, line, together, features), jnp.float32),
            pltpu.VMEM((2, line, n_row - 1, share, features), jnp.float32),
            pltpu.VMEM((2, line, share, features), jnp.bfloat16),
            dma((chunks,)),
            dma,
            dma((2,)),
            dma((2, line, CORES)),
            dma((2, line)),
            dma((2, line)),
            dma((2, line)),
            dma((2, line, n_row - 1)),
            dma((2, line, n_row - 1)),
            dma((line, n_row - 1)),
            dma((line, n_row - 1)),
            dma((line,)),
            dma((2, line, line)),
            dma((2, line, per_row, n_row)),
            dma((2, line)),
            dma((2, line, per_row)),
            dma((2, line, per_row)),
        ],
        compiler_params=pltpu.CompilerParams(
            collective_id=0, has_side_effects=True, vmem_limit_bytes=62 * 2**20
        ),
        name="gather",
    )(pruned_in, dense_in, weight, keep_bits)


def tiles_kernel(tokens, panels, cols, gram, cross):
    dims = (((0,), (0,)), ((), ()))
    right = cols[...]
    for m, out in enumerate((gram, cross)):
        product = lax.dot_general(panels[m], right, dims, preferred_element_type=jnp.float32)
        out[...] = product / tokens if tokens & (tokens - 1) else product * (1.0 / tokens)


def tiles(cols, panels):
    tokens, features = cols.shape
    height = panels.shape[2]
    step = block_of(height, (256, 128))
    out = jax.ShapeDtypeStruct((height, features), jnp.float32)
    return pl.pallas_call(
        functools.partial(tiles_kernel, tokens),
        grid=(height // step,),
        out_shape=(out, out),
        in_specs=[
            pl.BlockSpec((2, tokens, step), lambda i: (0, 0, i)),
            pl.BlockSpec((tokens, features), lambda i: (0, 0)),
        ],
        out_specs=(
            pl.BlockSpec((step, features), lambda i: (i, 0)),
            pl.BlockSpec((step, features), lambda i: (i, 0)),
        ),
        name="tiles",
    )(panels, cols)


def local(dense_in, pruned_in, weight, keep_bits):
    cols, panels = gather(pruned_in, dense_in, weight, keep_bits)
    return tiles(cols, panels)


def solution(mesh):
    in_specs = (P("col", "row"), P("col", "row"), P("row", "col"), P("col", "row"))
    out_specs = (P("row", "col"), P("row", "col"))
    return jax.shard_map(local, mesh=mesh, in_specs=in_specs, out_specs=out_specs, check_vma=False)
```

profile of v0, /device:TPU:7, one launch (start us, length us, event | category | flops | bytes accessed | tf_op | source)
XLA Modules:
  0.0 190.0 jit_solution(11416290024616780387)
XLA Ops:
  0.6 178.5 %gather.1 = (bf16[512,1024]{1,0:T(8,128)(2,1)}, bf16[2,512,2048]{2,1,0:T(8,128)(2,1)}) custom-call(bf16[64,7168]{1,0:T(8,128)(2,1)} %pruned_in.1, bf16[64,7168]{1,0:T(8,128)(2,1)} %dense_in.1, bf16[7168,1024]{1,0:T(8,128)(2,1)} %weight.1, s32[64,7168]{1,0:T(8,128)} %keep.1), custom_call_target="tpu_custom_call" | custom-call | tf_op jit(solution)/shard_map/gather/pallas_call | solution.py:367
  179.2 10.8 %tiles.1 = (f32[2048,1024]{1,0:T(8,128)}, f32[2048,1024]{1,0:T(8,128)}) custom-call(bf16[2,512,2048]{2,1,0:T(8,128)(2,1)} %get-tuple-element.4.panels, bf16[512,1024]{1,0:T(8,128)(2,1)} %get-tuple-element.5.cols), custom_call_target="tpu_custom_call" | custom-call | tf_op jit(solution)/shard_map/tiles/pallas_call | solution.py:421
where the time goes:
time: 192 us; the launch traced here: 190 us
  Pallas kernels  189 us (98%)
    pallas_call x1, Pallas kernels, gather(): pl.pallas_call(functools.partial(gather_kernel, n_row, n_col), out_shape=...  179 us
    pallas_call x1, Pallas kernels, tiles(): pl.pallas_call(functools.partial(tiles_kernel, tokens), grid=(height // s...  10.8 us

commit v1 on v0

--- a/solution.py
+++ b/solution.py
@@ -11,6 +11,8 @@
 CORES = 2
 FLAG_BITS = 16
 HALF_BITS = 8
+LAG = 1
+PAIR_LAG = 2
 
 
 def block_of(size, choices):
@@ -24,10 +26,10 @@
     n_row, n_col,
     pruned_in, dense_in, weight, keep,
     cols, panels,
-    xs, ws, flags, pick, part, heard, piece,
+    xs, ws, flags, pick, part, heard, posts,
     weight_sem, keep_sem, own_sem, x_recv, left_send, right_send, mate_send,
     sum_send, sum_recv, col_send, col_recv, col_own,
-    panel_send, panel_recv, panel_own, pair_send, pair_recv,
+    post_send, post_recv, flat_send, panel_recv, pair_send, pair_recv,
 ):
     rows, depth = pruned_in.shape
     features = weight.shape[1]
@@ -40,15 +42,22 @@
     z, core = col // CORES, lax.rem(col, CORES)
     other = 1 - core
     mate = (row, z * CORES + other)
-    home = col // per_row
-    slot = lax.rem(col, per_row)
 
     barrier = pltpu.get_barrier_semaphore()
-    for d in range(n_row):
-        for e in range(n_col):
-            if d or e:
-                peer = (lax.rem(row + d, n_row), lax.rem(col + e, n_col))
-                pl.semaphore_signal(barrier, inc=1, device_id=peer, device_id_type=MESH)
+    signal = functools.partial(pl.semaphore_signal, barrier, inc=1, device_id_type=MESH)
+
+    @pl.when(z > 0)
+    def _():
+        signal(device_id=(row, col - CORES))
+
+    @pl.when(z < line - 1)
+    def _():
+        signal(device_id=(row, col + CORES))
+
+    signal(device_id=mate)
+
+    for d in range(1, n_row):
+        signal(device_id=(lax.rem(row + d, n_row), col))
 
     chunk = block_of(depth, (512, 256, 128))
     chunks = depth // chunk
@@ -97,7 +106,7 @@
     def to_mate(m, q, source):
         return x_copy(m, q, core, source, mate, mate_send.at[m, q])
 
-    pl.semaphore_wait(barrier, n_row * n_col - 1)
+    pl.semaphore_wait(barrier, 2 + n_row - jnp.where(z == 0, 1, 0) - jnp.where(z == line - 1, 1, 0))
     for m in range(2):
         @pl.when(z > 0)
         def _():
@@ -203,7 +212,7 @@
 
     def col_copy(q, d):
         return pltpu.make_async_remote_copy(
-            src_ref=piece.at[0, q],
+            src_ref=posts.at[0, q, z],
             dst_ref=cols.at[token_rows(q, row)],
             send_sem=col_send.at[q, d - 1],
             recv_sem=col_recv.at[q, d - 1],
@@ -212,25 +221,84 @@
         )
 
     def col_local(q):
-        return pltpu.make_async_copy(piece.at[0, q], cols.at[token_rows(q, row)], col_own.at[q])
-
-    def panel_copy(m, q, j, source_row, at):
+        return pltpu.make_async_copy(posts.at[0, q, z], cols.at[token_rows(q, row)], col_own.at[q])
+
+    def post_copy(m, q, f, way):
         return pltpu.make_async_remote_copy(
-            src_ref=piece.at[m, q],
-            dst_ref=panels.at[m, token_rows(q, source_row), slot_columns(j)],
-            send_sem=panel_send.at[m, q, at],
-            recv_sem=panel_recv.at[m, q, j, source_row],
-            device_id=(home, at * CORES + core),
+            src_ref=posts.at[m, q, f],
+            dst_ref=posts.at[m, q, f],
+            send_sem=post_send.at[way, m, q, f],
+            recv_sem=post_recv.at[m, q, f],
+            device_id=(row, col + CORES * (2 * way - 1)),
             device_id_type=MESH,
         )
 
-    def panel_local(m, q):
-        return pltpu.make_async_copy(
-            piece.at[m, q], panels.at[m, token_rows(q, row), slot_columns(slot)], panel_own.at[m, q]
+    def can_go(way):
+        return z < line - 1 if way else z > 0
+
+    def panel_at(m, q, j, source_row):
+        return panels.at[m, token_rows(q, source_row), slot_columns(j)]
+
+    def flat_local(m, q, f):
+        j = lax.rem(f * CORES + core, per_row)
+        return pltpu.make_async_copy(posts.at[m, q, f], panel_at(m, q, j, row), flat_send.at[m, q, f])
+
+    def flat_copy(m, q, f, j, source_row):
+        return pltpu.make_async_remote_copy(
+            src_ref=posts.at[m, q, f],
+            dst_ref=panel_at(m, q, j, source_row),
+            send_sem=flat_send.at[m, q, f],
+            recv_sem=panel_recv.at[m, q, j, source_row],
+            device_id=((f * CORES + core) // per_row, col),
+            device_id_type=MESH,
         )
 
-    def is_self(at):
-        return (at == z) & (row == home)
+    def flat_own(f):
+        return (f * CORES + core) // per_row == row
+
+    def send_flat(m, q, f):
+        @pl.when(flat_own(f))
+        def _():
+            flat_local(m, q, f).start()
+
+        @pl.when(jnp.logical_not(flat_own(f)))
+        def _():
+            flat_copy(m, q, f, lax.rem(f * CORES + core, per_row), row).start()
+
+    def send_own(t):
+        s, m = t // 2, lax.rem(t, 2)
+
+        @pl.loop(0, 2)
+        def _(side):
+            q = position(s, side)
+
+            @pl.when(present(s, side, q))
+            def _():
+                for way in range(2):
+                    @pl.when(can_go(way))
+                    def _():
+                        post_copy(m, q, z, way).start()
+
+    def relay(t, d):
+        s, m = t // 2, lax.rem(t, 2)
+        for way in range(2):
+            f = z + d * (1 - 2 * way)
+
+            @pl.when((f >= 0) & (f < line))
+            def _():
+                @pl.loop(0, 2)
+                def _(side):
+                    q = f + s * (1 - 2 * side)
+
+                    @pl.when(present(s, side, q))
+                    def _():
+                        post_copy(m, q, f, way).wait_recv()
+
+                        @pl.when(can_go(way))
+                        def _():
+                            post_copy(m, q, f, way).start()
+
+                        send_flat(m, q, f)
 
     def settle(m, s):
         @pl.loop(0, 2)
@@ -243,17 +311,8 @@
                 for d in range(1, n_row):
                     sum_copy(m, q, d).wait_recv()
                     total = total + heard[m, q, d - 1]
-                piece[m, q] = total.astype(jnp.bfloat16)
-
-                @pl.loop(0, line)
-                def _(at):
-                    @pl.when(is_self(at))
-                    def _():
-                        panel_local(m, q).start()
-
-                    @pl.when(jnp.logical_not(is_self(at)))
-                    def _():
-                        panel_copy(m, q, slot, row, at).start()
+                posts[m, q, z] = total.astype(jnp.bfloat16)
+                send_flat(m, q, z)
 
                 @pl.when(m == 0)
                 def _():
@@ -264,9 +323,19 @@
     for m in range(2):
         own_copy(m).wait()
 
-    @pl.loop(0, 2 * line)
+    last = 2 * line - 1
+    at_end = (z == 0) | (z == line - 1)
+
+    @pl.loop(0, last + 1)
     def _(t):
         s, m = t // 2, lax.rem(t, 2)
+
+        @pl.when((t == last) & at_end)
+        def _():
+            @pl.loop(0, last - 1)
+            def _(before):
+                send_own(before)
+
         arrive(m, s)
         multiply(m, s)
 
@@ -274,7 +343,15 @@
         def _():
             settle(1 - m, (t - 1) // 2)
 
+    @pl.when(at_end)
+    def _():
+        send_own(last - 1)
+
     settle(1, line - 1)
+
+    @pl.when(at_end)
+    def _():
+        send_own(last)
 
     def comes_here(j):
         return lax.rem(row * per_row + j, CORES) == core
@@ -293,8 +370,7 @@
             device_id_type=MESH,
         )
 
-    @pl.loop(0, 2 * line)
-    def _(t):
+    def pair_up(t):
         s, m = t // 2, lax.rem(t, 2)
 
         @pl.loop(0, 2)
@@ -306,17 +382,35 @@
                 @pl.when(present(s, side, q) & comes_here(j))
                 def _():
                     for source_row in range(n_row):
-                        here = (origin == z) & (row == source_row)
-
-                        @pl.when(here)
+                        @pl.when(row == source_row)
                         def _():
-                            panel_local(m, q).wait()
-
-                        @pl.when(jnp.logical_not(here))
+                            flat_local(m, q, origin).wait()
+
+                        @pl.when(row != source_row)
                         def _():
-                            panel_copy(m, q, j, source_row, z).wait_recv()
+                            flat_copy(m, q, origin, j, source_row).wait_recv()
 
                     pair_copy(m, q, j).start()
+
+    behind = LAG * (line - 1) + PAIR_LAG
+
+    @pl.loop(0, last + 1 + behind)
+    def _(u):
+        @pl.when(jnp.logical_not(at_end) & (u <= last))
+        def _():
+            send_own(u)
+
+        @pl.loop(1, line)
+        def _(d):
+            t = u - LAG * d
+
+            @pl.when((t >= 0) & (t <= last))
+            def _():
+                relay(t, d)
+
+        @pl.when(u >= behind)
+        def _():
+            pair_up(u - behind)
 
     @pl.loop(0, line)
     def _(q):
@@ -335,10 +429,18 @@
                     pair_copy(m, q, j).wait_recv()
 
             @pl.loop(0, line)
-            def _(at):
-                @pl.when(jnp.logical_not(is_self(at)))
-                def _():
-                    panel_copy(m, q, slot, row, at).wait_send()
+            def _(f):
+                @pl.when(jnp.logical_not(flat_own(f)))
+                def _():
+                    flat_copy(m, q, f, lax.rem(f * CORES + core, per_row), row).wait_send()
+
+                @pl.when((z > 0) & (f >= z))
+                def _():
+                    post_copy(m, q, f, 0).wait_send()
+
+                @pl.when((z < line - 1) & (f <= z))
+                def _():
+                    post_copy(m, q, f, 1).wait_send()
 
             for d in range(1, n_row):
                 sum_copy(m, q, d).wait_send()
@@ -379,7 +481,7 @@
             pltpu.VMEM((2 * words, features), jnp.bfloat16),
             pltpu.VMEM((2, line, together, features), jnp.float32),
             pltpu.VMEM((2, line, n_row - 1, share, features), jnp.float32),
-            pltpu.VMEM((2, line, share, features), jnp.bfloat16),
+            pltpu.VMEM((2, line, line, share, features), jnp.bfloat16),
             dma((chunks,)),
             dma,
             dma((2,)),
@@ -392,9 +494,10 @@
             dma((line, n_row - 1)),
             dma((line, n_row - 1)),
             dma((line,)),
+            dma((2, 2, line, line)),
+            dma((2, line, line)),
             dma((2, line, line)),
             dma((2, line, per_row, n_row)),
-            dma((2, line)),
             dma((2, line, per_row)),
             dma((2, line, per_row)),
         ],
@@ -416,7 +519,7 @@
 def tiles(cols, panels):
     tokens, features = cols.shape
     height = panels.shape[2]
-    step = block_of(height, (256, 128))
+    step = block_of(height, (512, 256, 128))
     out = jax.ShapeDtypeStruct((height, features), jnp.float32)
     return pl.pallas_call(
         functools.partial(tiles_kernel, tokens),

time: 192 us -> 181 us (0.943)
  Pallas kernels: 189 us -> 180 us
    pallas_call x1, Pallas kernels: 179 us -> 171 us  [gather(): pl.pallas_call(functools.partial(gather_kernel, n_row, n_col), out_shape=...]
where the time goes in v1:
time: 181 us
  Pallas kernels  180 us (99%)
    pallas_call x1, Pallas kernels, gather(): pl.pallas_call(functools.partial(gather_kernel, n_row, n_col), out_shape=...  171 us
    pallas_call x1, Pallas kernels, tiles(): pl.pallas_call(functools.partial(tiles_kernel, tokens), grid=(height // s...  9.08 us

profile of v1, /device:TPU:7, one launch (start us, length us, event | category | flops | bytes accessed | tf_op | source)
XLA Modules:
  0.0 180.7 jit_solution(4211319977032348740)
XLA Ops:
  0.6 171.0 %gather.1 = (bf16[512,1024]{1,0:T(8,128)(2,1)}, bf16[2,512,2048]{2,1,0:T(8,128)(2,1)}) custom-call(bf16[64,7168]{1,0:T(8,128)(2,1)} %pruned_in.1, bf16[64,7168]{1,0:T(8,128)(2,1)} %dense_in.1, bf16[7168,1024]{1,0:T(8,128)(2,1)} %weight.1, s32[64,7168]{1,0:T(8,128)} %keep.1), custom_call_target="tpu_custom_call" | custom-call | tf_op jit(solution)/shard_map/gather/pallas_call | solution.py:469
  171.7 9.1 %tiles.1 = (f32[2048,1024]{1,0:T(8,128)}, f32[2048,1024]{1,0:T(8,128)}) custom-call(bf16[2,512,2048]{2,1,0:T(8,128)(2,1)} %get-tuple-element.4.panels, bf16[512,1024]{1,0:T(8,128)(2,1)} %get-tuple-element.5.cols), custom_call_target="tpu_custom_call" | custom-call | tf_op jit(solution)/shard_map/tiles/pallas_call | solution.py:524

commit v2 on v1

--- a/solution.py
+++ b/solution.py
@@ -12,6 +12,7 @@
 FLAG_BITS = 16
 HALF_BITS = 8
 LAG = 1
+EARLY = 3
 PAIR_LAG = 2
 
 
@@ -347,11 +348,6 @@
     def _():
         send_own(last - 1)
 
-    settle(1, line - 1)
-
-    @pl.when(at_end)
-    def _():
-        send_own(last)
 
     def comes_here(j):
         return lax.rem(row * per_row + j, CORES) == core
@@ -394,8 +390,7 @@
 
     behind = LAG * (line - 1) + PAIR_LAG
 
-    @pl.loop(0, last + 1 + behind)
-    def _(u):
+    def advance(u):
         @pl.when(jnp.logical_not(at_end) & (u <= last))
         def _():
             send_own(u)
@@ -411,6 +406,20 @@
         @pl.when(u >= behind)
         def _():
             pair_up(u - behind)
+
+    @pl.loop(0, EARLY)
+    def _(u):
+        advance(u)
+
+    settle(1, line - 1)
+
+    @pl.when(at_end)
+    def _():
+        send_own(last)
+
+    @pl.loop(EARLY, last + 1 + behind)
+    def _(u):
+        advance(u)
 
     @pl.loop(0, line)
     def _(q):

time: 181 us -> 181 us (level)
  no operation moved by 1% of the time
where the time goes in v2:
time: 181 us
  Pallas kernels  180 us (99%)
    pallas_call x1, Pallas kernels, gather(): pl.pallas_call(functools.partial(gather_kernel, n_row, n_col), out_shape=...  171 us
    pallas_call x1, Pallas kernels, tiles(): pl.pallas_call(functools.partial(tiles_kernel, tokens), grid=(height // s...  9.08 us

profile of v2, /device:TPU:7, one launch (start us, length us, event | category | flops | bytes accessed | tf_op | source)
XLA Modules:
  0.0 180.8 jit_solution(9918263074275121754)
XLA Ops:
  0.6 171.1 %gather.1 = (bf16[512,1024]{1,0:T(8,128)(2,1)}, bf16[2,512,2048]{2,1,0:T(8,128)(2,1)}) custom-call(bf16[64,7168]{1,0:T(8,128)(2,1)} %pruned_in.1, bf16[64,7168]{1,0:T(8,128)(2,1)} %dense_in.1, bf16[7168,1024]{1,0:T(8,128)(2,1)} %weight.1, s32[64,7168]{1,0:T(8,128)} %keep.1), custom_call_target="tpu_custom_call" | custom-call | tf_op jit(solution)/shard_map/gather/pallas_call | solution.py:478
  171.7 9.1 %tiles.1 = (f32[2048,1024]{1,0:T(8,128)}, f32[2048,1024]{1,0:T(8,128)}) custom-call(bf16[2,512,2048]{2,1,0:T(8,128)(2,1)} %get-tuple-element.4.panels, bf16[512,1024]{1,0:T(8,128)(2,1)} %get-tuple-element.5.cols), custom_call_target="tpu_custom_call" | custom-call | tf_op jit(solution)/shard_map/tiles/pallas_call | solution.py:533
